TPU v7x, 256 devices: a whole 4x4x8 slice. The times are simulated.
256 devices in a mesh: vocab: 64 (over z, y, core), layer: 4 (over x).
Axes of the slice: x: 4, y: 4, z: 8, core: 2. Of those that a mesh axis runs over, the one named last changes fastest.
Arguments:
- residual: bfloat16 [1024, 8192], P('layer', 'vocab'), may hold values from -40 to 40
- gain: bfloat16 [1, 8192], P(None, 'vocab'), may hold values from 0.25 to 1.75
- unembed: bfloat16 [8192, 128256], P(None, ('vocab', 'layer')), may hold values from -0.22097087 to 0.22097087
Outputs:
- log_probs: float32 [1024, 128256], P('layer', 'vocab')
All inputs are finite; a program needn't handle non-finite values.
Results may differ from a plain program's by a relative error of at most 0.0003.
Values may be sent and summed in bfloat16 or wider, within the bound.
A program may use at most 128 MiB of HBM per device.

v0:
```python
import jax
import jax.numpy as jnp
from jax import lax
from jax.sharding import Mesh
from jax.sharding import PartitionSpec as P

D = 8192
VOCAB = ("vocab_0", "vocab_1", "vocab_2")
VOCAB_LAYER = ("vocab_0", "vocab_1", "vocab_2", "layer")


def sent_to_all(shard, axis):
    length = lax.axis_size(axis)
    return lax.all_to_all(
        jnp.broadcast_to(shard[None], (length, *shard.shape)), axis, 0, 0, tiled=True
    )


def joined_along(parts, dim):
    shape = list(parts.shape[1:])
    shape[dim] *= parts.shape[0]
    return jnp.moveaxis(parts, 0, dim).reshape(shape)


def gathered_copies(shard, axis, dim):
    parts = sent_to_all(shard, axis)
    return joined_along(parts, dim)


def collected_together(shard, axis):
    leaves = jax.tree.leaves(shard)
    order = sorted(range(len(leaves)), key=lambda k: -leaves[k].size)
    width = (1, *leaves[order[0]].shape)[-1]
    lines = [
        jnp.pad(leaves[k].reshape(-1), (0, -leaves[k].size % width)).reshape(-1, width)
        for k in order
    ]
    both, at, found = (lax.all_gather(jnp.concatenate(lines), axis), 0, {})
    for k, line in zip(order, lines):
        piece = both[:, at : at + len(line)].reshape(len(both), -1)
        found[k] = piece[:, : leaves[k].size].reshape(-1, *leaves[k].shape)
        at += len(line)
    numbers = iter(range(len(leaves)))
    return jax.tree.map(lambda _: found[next(numbers)], shard)


def merged_by_axis(shard, axes, combine):
    for axis in axes:
        pieces = collected_together(shard, axis)
        shard = jax.tree.map(lambda part: part[0], pieces)
        for k in range(1, lax.axis_size(axis)):
            shard = combine(shard, jax.tree.map(lambda part: part[k], pieces))
    return shard


def combine_pairs(earlier, later):
    highest = jnp.maximum(earlier[0], later[0])
    totals = earlier[1] * jnp.exp(earlier[0] - highest) + later[1] * jnp.exp(later[0] - highest)
    return (highest, totals)


def local(residual, gain, unembed):
    all_pieces = gathered_copies(residual, "layer", 0)
    portion = lax.all_gather(all_pieces, VOCAB, axis=1, tiled=True)
    gain_piece = lax.all_gather(gain, VOCAB, axis=1, tiled=True)
    widened = portion.astype(jnp.float32)
    scaled = (widened * gain_piece.astype(jnp.float32)).astype(jnp.bfloat16)
    totals = jnp.dot(scaled, unembed, preferred_element_type=jnp.float32)
    products = totals
    squares = jnp.sum(widened * widened, axis=1)
    inverse = lax.rsqrt(squares / D + 1e-05)
    logits = products * inverse[:, None]
    local_max = jnp.max(logits, axis=1)
    local_sums = jnp.sum(jnp.exp(logits - local_max[:, None]), axis=1)
    highest, totals = merged_by_axis((local_max, local_sums), VOCAB_LAYER, combine_pairs)
    lse = highest + jnp.log(totals)
    log_values = logits - lse[:, None]
    return lax.all_to_all(log_values, "layer", split_axis=0, concat_axis=1, tiled=True)


def solution(mesh):
    torus = Mesh(
        mesh.devices.reshape(8, 4, 2, mesh.shape["layer"]),
        ("vocab_0", "vocab_1", "vocab_2", "layer"),
    )
    placed = (P("layer", VOCAB), P(None, VOCAB), P(None, VOCAB_LAYER))
    return jax.shard_map(
        local, mesh=torus, in_specs=placed, out_specs=P("layer", VOCAB), check_vma=False
    )
```

profile of v0, /device:TPU:2, one launch (start us, length us, event | category | flops | bytes accessed | tf_op | source)
XLA Modules:
  0.0 237.0 jit_solution(9960523296780332868)
XLA Ops:
  6.5 0.0 all-gather.10.cloned.1.call-start
  6.5 0.9 broadcast_in_dim.2
  7.4 10.5 %all_to_all.24 = bf16[4,256,128]{2,1,0:T(8,128)(2,1)} all-to-all(bf16[4,256,128]{2,1,0:T(8,128)(2,1)S(1)} %broadcast_in_dim.2), channel_id=1, replica_groups=mesh['vocab_0'=8,'vocab_1'=4,'vocab_2'=2,'layer'=4] {'layer'}, dimensions={0} | all-to-all | bytes 524288 | tf_op jit(solution)/shard_map/all_to_all | solution.py:14
  17.9 0.0 all-gather.10.cloned.1.call-update
  18.0 42.4 %all_gather.31 = bf16[1,8192]{1,0:T(2,128)(2,1)S(1)} all-gather(bf16[1,128]{1,0:T(2,128)(2,1)} %param.4), channel_id=1, replica_groups=mesh['vocab_0'=8,'vocab_1'=4,'vocab_2'=2,'layer'=4] {'vocab_0','vocab_1'..., dimensions={1}, use_global_device_ids=true | all-gather | bytes 16640 | tf_op jit(solution)/shard_map/all_gather | solution.py:65
  60.4 65.0 %all-gather.10.cloned.1.call-done = bf16[1024,8192]{1,0:T(8,128)(2,1)} async-done(((bf16[1024,128]{1,0:T(8,128)(2,1)}), bf16[1024,8192]{1,0:T(8,128)(2,1)}) %all-gather.10.cloned.1.call-update) | async-done | bytes 16777232 | tf_op jit(solution)/shard_map/all_gather | solution.py:64
  125.4 7.2 %fusion.1 = f32[1024]{0:T(1024)S(1)} fusion(bf16[1024,8192]{1,0:T(8,128)(2,1)} %all-gather.10.cloned.1.call-done), kind=kLoop, calls=%fused_computation.3 | loop fusion | flops 25164800 | bytes 16781312 | tf_op jit(solution)/shard_map/reduce_sum | solution.py:70
  132.6 14.4 %multiply_reduce_fusion = (f32[1024]{0:T(1024)S(1)}, f32[1024,501]{0,1:T(8,128)S(1)}) fusion(f32[1024]{0:T(1024)S(1)} %add_rsqrt_fusion, bf16[8192,501]{0,1:T(8,128)(2,1)} %param.5, bf16[1024,8192]{1,0:T(8,128)(2,1)} %all-gather.10.cloned.1.call-done, f32[8192]{0:T(1024)S(1)} %bitcast.282), kind=kOutput, calls=%fused_computation.8 | convolution fusion | flops 8431576064 | bytes 27078656 | tf_op jit(solution)/shard_map/dot_general | solution.py:68
  147.0 0.4 exponential_reduce_fusion
  147.3 24.6 %all-gather.4 = f32[8,2,1024]{2,1,0:T(2,128)S(1)} all-gather(f32[1,2,1024]{2,1,0:T(2,128)S(1)} %maximum_bitcast_fusion), channel_id=2, replica_groups=mesh['vocab_0'=8,'vocab_1'=4,'vocab_2'=2,'layer'=4] {'vocab_0'}, dimensions={0}, use_global_device_ids=true | all-gather | bytes 73728 | tf_op jit(solution)/shard_map/all_gather | solution.py:38
  171.9 0.1 fusion.18
  172.1 11.9 %all-gather.5 = f32[4,2,1024]{2,1,0:T(2,128)S(1)} all-gather(f32[1,2,1024]{2,1,0:T(2,128)S(1)} %maximum_bitcast_fusion.1), channel_id=3, replica_groups=mesh['vocab_0'=8,'vocab_1'=4,'vocab_2'=2,'layer'=4] {'vocab_1'}, dimensions={0}, use_global_device_ids=true | all-gather | bytes 40960 | tf_op jit(solution)/shard_map/all_gather | solution.py:38
  184.0 0.1 fusion.9
  184.1 1.8 all-gather.6
  185.9 11.9 %all-gather.7 = f32[4,2,1024]{2,1,0:T(2,128)S(1)} all-gather(f32[1,2,1024]{2,1,0:T(2,128)S(1)} %maximum_bitcast_fusion.3), channel_id=5, replica_groups=mesh['vocab_0'=8,'vocab_1'=4,'vocab_2'=2,'layer'=4] {'layer'}, dimensions={0}, use_global_device_ids=true | all-gather | bytes 40960 | tf_op jit(solution)/shard_map/all_gather | solution.py:38
  197.9 0.3 multiply_subtract_fusion
  198.2 2.2 all_to_all.18
  200.4 2.0 copy.7
  202.4 26.3 %all_to_all.25 = f32[4,256,501]{1,2,0:T(8,128)S(1)} all-to-all(f32[4,256,501]{1,2,0:T(8,128)S(1)} %copy.7), channel_id=1, replica_groups=mesh['vocab_0'=8,'vocab_1'=4,'vocab_2'=2,'layer'=4] {'layer'}, dimensions={0} | all-to-all | bytes 4104192 | tf_op jit(solution)/shard_map/all_to_all | solution.py:78
  228.6 1.5 all_to_all.21
  (9 shorter events, 0.2 us)
Async XLA Ops:
  6.5 118.8 %all-gather.10.cloned.1.call-start = ((), (), s32[]{:S(2)}) async-start(), calls=%async_computation.2 | async-start | bytes 17039360 | tf_op jit(solution)/shard_map/all_gather | solution.py:64
Sparse Core Ops, SparseCore 0:
  18.1 107.2 all-gather.9
where the time goes:
time: 237 us
  blocking collectives  129 us (54%)
  waiting for transfers between devices  65 us (27%)
  matrix products  14.4 us (6%)
  between operations  13.5 us (6%)
  other arithmetic  8.09 us (3%)
  local copies, waits for them, and re-layouts  6.63 us (3%)
    all_gather x1, waiting for transfers between devices, local(): portion = lax.all_gather(all_pieces, VOCAB, axis=1, tiled=True)  65 us
    all_gather x4, blocking collectives, collected_together(): both, at, found = (lax.all_gather(jnp.concatenate(lines), axis), 0, {})  50.3 us
    all_gather x1, blocking collectives, local(): gain_piece = lax.all_gather(gain, VOCAB, axis=1, tiled=True)  42.4 us
    all_to_all x1, blocking collectives, local(): lax.all_to_all(log_values, 'layer', split_axis=0, concat_axis=1, tiled=True)  26.3 us
    dot_general x1, matrix products, local(): totals = jnp.dot(scaled, unembed, preferred_element_type=jnp.float32)  14.4 us
    all_to_all x1, blocking collectives, sent_to_all(): lax.all_to_all(jnp.broadcast_to(shard[None], (length, *shard.shape)), axi...  10.5 us
    reduce_sum x1, other arithmetic, local(): squares = jnp.sum(widened * widened, axis=1)  7.18 us
    all_to_all x3, local copies, waits for them, and re-layouts, local(): lax.all_to_all(log_values, 'layer', split_axis=0, concat_axis=1, tiled=True)  5.73 us
  transfers between devices with their start and end apart: 1, of which 1 were waited for; matrix products, arithmetic and copies ran while one was open for 0% of the time, Pallas kernels for 0%

commit v1 on v0

v1 whole, which is shorter than its diff:
```python
import jax
import jax.numpy as jnp
from jax import lax
from jax.experimental import pallas as pl
from jax.experimental.pallas import tpu as pltpu
from jax.sharding import Mesh
from jax.sharding import PartitionSpec as P

D = 8192
MESH = pl.DeviceIdType.MESH
AXES = ("z", "y", "c", "x")
NX, NZ, NY = 4, 8, 4
ROWS, FEAT, COLS = 256, 128, 501
WIDE = 512

HOPS = (
    641, 284, 388, 515, 160, 96, 3492, 3169, 3717, 3359, 3260, 3591,
    4376, 4707, 4220, 4765, 4488, 4257, 5312, 5762, 5220, 5667, 6537, 6247,
    6456, 6790, 6695, 6335, 7451, 7272, 7563, 7933, 7778, 7336, 8468, 8933,
    8319, 8588, 8771, 8412, 9766, 9881, 9643, 9524, 9284, 9405, 10639, 10345,
    10937, 10409, 10814, 10617, 11934, 11543, 11661, 11883, 11436, 11335, 12404, 12603,
    12491, 12949, 12744, 12826, 14010, 13584, 13715, 13528, 13838, 13423, 15029, 14509,
    14768, 14712, 14890, 14455, 15564, 16106, 15633, 15894, 15482, 15791, 16501, 16876,
    17097, 16752, 16563, 16951, 17901, 17613, 17718, 17518, 18058, 17938, 19121, 18931,
    19067, 18640, 18519, 18722, 19535, 20214, 20018, 19838, 19942, 19667, 20805, 20654,
    20978, 20593, 21198, 21029, 21972, 22225, 21855, 21589, 21722, 22107, 22742, 23114,
    23261, 22598, 23873, 24281, 23634, 24130, 23774,
)
LAG = 3
STEPS = ((1, 0, 0), (-1, 0, 0), (0, 1, 0), (0, -1, 0), (0, 0, 1), (0, 0, -1))


def plan():
    arrive = {0: 0}
    for hop in HOPS:
        arrive[hop % 128] = hop // 1024 + LAG
    last = max(arrive.values())
    rounds = []
    for r in range(last + 2):
        takes = [t for t in arrive if arrive[t] == r and t != 0]
        hops = [(hop // 128 % 8, hop % 128) for hop in HOPS if hop // 1024 == r]
        groups = [
            g for g in range(32) if max(arrive[g * 4 + k] for k in range(4)) + 1 == r
        ]
        rounds.append((takes, hops, groups))
    return rounds


def offset_of(t):
    return t // 32, t // 4 % 8, t % 4


def kernel(
    res_ref, gain_ref, unembed_ref, out_ref,
    held, weights, acc, logits, ssq_a, ssq_b, st_a, st_b,
    w_sem, hop_send, hop_recv, pair_send, pair_recv,
    blk_send, blk_recv, sq_send, sq_recv, st_send, st_recv,
):
    z, y, c, x = (lax.axis_index(a) for a in AXES)

    def at(dx, dz, dy, dc=0):
        return (
            lax.rem(z + dz % NZ, NZ), lax.rem(y + dy % NY, NY),
            lax.rem(c + dc, 2), lax.rem(x + dx % NX, NX),
        )

    def slot(dx, dz, dy):
        zz, yy, _, xx = at(dx, dz, dy)
        return (xx * NZ + zz) * NY + yy

    load = pltpu.make_async_copy(unembed_ref, weights, w_sem)
    load.start()

    widened = res_ref[...].astype(jnp.float32)
    mine = slot(0, 0, 0)
    held[c, mine] = (widened * gain_ref[...].astype(jnp.float32)).astype(jnp.bfloat16)
    squares = jnp.sum(jnp.transpose(widened * widened), axis=0, keepdims=True)
    ssq_a[0] = jnp.broadcast_to(squares, (8, ROWS))

    barrier = pltpu.get_barrier_semaphore()
    near = [at(*step) for step in STEPS] + [at(0, 0, 0, 1)]
    for device in near:
        pl.semaphore_signal(barrier, inc=1, device_id=device, device_id_type=MESH)
    pl.semaphore_wait(barrier, len(near))

    def send(src, dst, send_sem, recv_sem, device):
        copy = pltpu.make_async_remote_copy(
            src_ref=src, dst_ref=dst, send_sem=send_sem, recv_sem=recv_sem,
            device_id=device, device_id_type=MESH,
        )
        copy.start()
        return copy

    def pair_send_of(t):
        s = slot(*offset_of(t))
        send(held.at[c, s], held.at[c, s], pair_send.at[t], pair_recv.at[t], at(0, 0, 0, 1))

    def landed(ref, sem):
        pltpu.make_async_copy(ref, ref, sem).wait()

    def exchange(buf, send_sem, recv_sem, places):
        copies = [
            send(buf.at[0], buf.at[k + 1], send_sem.at[k], recv_sem.at[k], place)
            for k, place in enumerate(places)
        ]
        return copies

    plane = [at(0, 0, dy, dc) for dy in range(NY) for dc in range(2) if dy or dc]
    column = [at(0, dz, 0) for dz in range(1, NZ)]

    pair_send_of(0)
    acc[...] = jnp.zeros_like(acc)
    load.wait()

    def multiply(g):
        dx, dz = g // 8, g % 8
        xx, zz = lax.rem(x + dx, NX), lax.rem(z + dz, NZ)

        @pl.loop(0, NY)
        def _(dy):
            yy = lax.rem(y + dy, NY)
            s = (xx * NZ + zz) * NY + yy
            landed(held.at[1 - c, s], pair_recv.at[g * NY + dy])
            both = jnp.concatenate([held[0, s], held[1, s]], axis=1)
            start = pl.multiple_of((zz * NY + yy) * (2 * FEAT), 2 * FEAT)
            acc[xx] += jnp.dot(
                both, weights[pl.ds(start, 2 * FEAT), :], preferred_element_type=jnp.float32
            )

    done = {dx: 0 for dx in range(NX)}
    blocks = []
    columns_started = None
    planes_started = None
    for takes, hops, groups in plan():
        for t in takes:
            s = slot(*offset_of(t))
            landed(held.at[c, s], hop_recv.at[t])
            pair_send_of(t)
        for d, t in hops:
            dx, dz, dy = (a + b for a, b in zip(offset_of(t), STEPS[d]))
            s = slot(dx, dz, dy)
            send(held.at[c, s], held.at[c, s], hop_send.at[t], hop_recv.at[t], at(*STEPS[d]))
        for g in groups:
            multiply(g)
            if g == 0:
                planes_started = exchange(ssq_a, sq_send.at[0], sq_recv.at[0], plane)
            dx = g // 8
            done[dx] += 1
            if done[dx] == 8 and dx:
                xx = lax.rem(x + dx, NX)
                blocks.append(
                    send(acc.at[xx], logits.at[x], blk_send.at[dx - 1], blk_recv.at[dx - 1], at(dx, 0, 0))
                )

    for copy in planes_started:
        copy.wait()
    ssq_b[0] = jnp.sum(ssq_a[...], axis=0)
    for copy in exchange(ssq_b, sq_send.at[1], sq_recv.at[1], column):
        copy.wait()
    inverse = lax.rsqrt(jnp.sum(ssq_b[...], axis=0) / D + 1e-05)

    def to_column(lines):
        tall = jnp.concatenate([lines] * (FEAT // 8), axis=0)
        return jnp.transpose(tall)

    inverse_column = to_column(inverse)[:, :1]
    logits[x] = acc[x]
    for copy in blocks:
        copy.wait()

    lane = lax.broadcasted_iota(jnp.int32, (1, COLS), 1)
    del lane
    highest = jnp.full((ROWS, 1), -jnp.inf, jnp.float32)
    for k in range(NX):
        scaled = logits[k] * inverse_column
        logits[k] = scaled
        highest = jnp.maximum(highest, jnp.max(scaled, axis=1, keepdims=True))
    total = jnp.zeros((ROWS, 1), jnp.float32)
    for k in range(NX):
        total = total + jnp.sum(jnp.exp(logits[k] - highest), axis=1, keepdims=True)

    lanes = lax.broadcasted_iota(jnp.int32, (ROWS, FEAT), 1)
    packed = jnp.where(lanes == 0, highest, total)
    st_a[0] = jnp.transpose(packed)[:8]

    def merged(buf):
        top = buf[0][:1]
        for k in range(1, 8):
            top = jnp.maximum(top, buf[k][:1])
        add = jnp.zeros_like(top)
        for k in range(8):
            add = add + buf[k][1:2] * jnp.exp(buf[k][:1] - top)
        return top, add

    for copy in exchange(st_a, st_send.at[0], st_recv.at[0], plane):
        copy.wait()
    top, add = merged(st_a)
    line = lax.broadcasted_iota(jnp.int32, (8, ROWS), 0)
    st_b[0] = jnp.where(line == 0, top, add)
    for copy in exchange(st_b, st_send.at[1], st_recv.at[1], column):
        copy.wait()
    top, add = merged(st_b)
    lse = to_column(jnp.broadcast_to(top + jnp.log(add), (8, ROWS)))[:, :1]
    for k in range(NX):
        out_ref[:, COLS * k : COLS * (k + 1)] = logits[k] - lse

    @pl.loop(0, 128)
    def _(t):
        landed(held.at[c, t], pair_send.at[t])

    @pl.loop(1, 128)
    def _(t):
        landed(held.at[c, t], hop_send.at[t])


def local(residual, gain, unembed):
    f32, bf16 = jnp.float32, jnp.bfloat16
    vmem = pl.BlockSpec(memory_space=pltpu.VMEM)
    dma = pltpu.SemaphoreType.DMA
    return pl.pallas_call(
        kernel,
        name="lens",
        out_shape=jax.ShapeDtypeStruct((ROWS, NX * COLS), f32),
        in_specs=[vmem, vmem, pl.BlockSpec(memory_space=pl.ANY)],
        out_specs=vmem,
        scratch_shapes=[
            pltpu.VMEM((2, NX * NZ * NY, ROWS, FEAT), bf16),
            pltpu.VMEM((D, COLS), bf16),
            pltpu.VMEM((NX, ROWS, COLS), f32),
            pltpu.VMEM((NX, ROWS, COLS), f32),
            pltpu.VMEM((8, 8, ROWS), f32),
            pltpu.VMEM((8, 8, ROWS), f32),
            pltpu.VMEM((8, 8, ROWS), f32),
            pltpu.VMEM((8, 8, ROWS), f32),
            dma, dma((128,)), dma((128,)), dma((128,)), dma((128,)),
            dma((3,)), dma((3,)), dma((2, 7)), dma((2, 7)), dma((2, 7)), dma((2, 7)),
        ],
        compiler_params=pltpu.CompilerParams(
            collective_id=0, has_side_effects=True, vmem_limit_bytes=60 * 1024 * 1024
        ),
    )(residual, gain, unembed)


def solution(mesh):
    torus = Mesh(mesh.devices.reshape(NZ, NY, 2, mesh.shape["layer"]), AXES)
    planes = ("z", "y", "c")
    return jax.shard_map(
        local,
        mesh=torus,
        in_specs=(P("x", planes), P(None, planes), P(None, (*planes, "x"))),
        out_specs=P("x", planes),
        check_vma=False,
    )
```

time: 237 us -> 113 us (0.48)
  blocking collectives: 129 us -> 0 us
  Pallas kernels: 0 us -> 97.6 us
  waiting for transfers between devices: 65 us -> 0 us
  matrix products: 14.4 us -> 0 us
  between operations: 13.5 us -> 0.01 us
  local copies, waits for them, and re-layouts: 6.63 us -> 14.8 us
  other arithmetic: 8.09 us -> 0 us
    pallas_call x0 -> x1, Pallas kernels: none -> 97.6 us  [local(): pl.pallas_call(kernel, name='lens', out_shape=jax.ShapeDtypeStruct((ROWS,...]
    all_gather x5 -> x0, blocking collectives: 92.7 us -> none  [the longest x4 50.3 us: collected_together(): both, at, found = (lax.all_gather(jnp.concatenate(lines), axis), 0, {})]
    all_gather x1 -> x0, waiting for transfers between devices: 65 us -> none  [local(): portion = lax.all_gather(all_pieces, VOCAB, axis=1, tiled=True)]
    all_to_all x2 -> x0, blocking collectives: 36.8 us -> none  [the longest x1 26.3 us: local(): lax.all_to_all(log_values, 'layer', split_axis=0, concat_axis=1, tiled=True)]
    dot_general x1 -> x0, matrix products: 14.4 us -> none  [local(): totals = jnp.dot(scaled, unembed, preferred_element_type=jnp.float32)]
    unnamed x0 -> x1, local copies, waits for them, and re-layouts: none -> 11.9 us
    reduce_sum x2 -> x0, other arithmetic: 7.55 us -> none  [the longest x1 7.18 us: local(): squares = jnp.sum(widened * widened, axis=1)]
    all_to_all x3 -> x0, local copies, waits for them, and re-layouts: 5.73 us -> none  [local(): lax.all_to_all(log_values, 'layer', split_axis=0, concat_axis=1, tiled=True)]
  transfers between devices with their start and end apart: 1 -> 0, of which waited for: 1 -> 0; matrix products, arithmetic and copies ran while one was open for 0% -> 0% of each run, Pallas kernels for 0% -> 0%
where the time goes in v1:
time: 113 us; the launch traced here: 112 us
  Pallas kernels  97.6 us (86%)
  local copies, waits for them, and re-layouts  14.8 us (13%)
    pallas_call x1, Pallas kernels, local(): pl.pallas_call(kernel, name='lens', out_shape=jax.ShapeDtypeStruct((ROWS,...  97.6 us
    unnamed x1, local copies, waits for them, and re-layouts  11.9 us
    pallas_call x1, local copies, waits for them, and re-layouts, local(): pl.pallas_call(kernel, name='lens', out_shape=jax.ShapeDtypeStruct((ROWS,...  2.87 us

profile of v1, /device:TPU:2, one launch (start us, length us, event | category | flops | bytes accessed | tf_op | source)
XLA Modules:
  0.0 112.4 jit_solution(12306982556758293152)
XLA Ops:
  0.0 11.9 %copy.4.unembed_ref = bf16[8192,501]{1,0:T(8,128)(2,1)} copy(bf16[8192,501]{0,1:T(8,128)(2,1)} %param.5) | data formatting | bytes 16416768 | tf_op args[2]
  11.9 97.6 %lens.1 = f32[256,2004]{1,0:T(8,128)} custom-call(bf16[256,128]{1,0:T(8,128)(2,1)} %res_ref.1, bf16[1,128]{1,0:T(2,128)(2,1)} %gain_ref.1, bf16[8192,501]{1,0:T(8,128)(2,1)} %copy.4.unembed_ref), custom_call_target="tpu_custom_call" | custom-call | tf_op jit(solution)/shard_map/lens/pallas_call | solution.py:220
  109.5 2.9 %copy.5 = f32[256,2004]{0,1:T(8,128)} copy(f32[256,2004]{1,0:T(8,128)} %lens.1) | data formatting | bytes 4104192 | tf_op jit(solution)/shard_map/lens/pallas_call | solution.py:220

commit v2 on v1

--- a/solution.py
+++ b/solution.py
@@ -11,7 +11,7 @@
 AXES = ("z", "y", "c", "x")
 NX, NZ, NY = 4, 8, 4
 ROWS, FEAT, COLS = 256, 128, 501
-WIDE = 512
+SKIP = ()
 
 HOPS = (
     641, 284, 388, 515, 160, 96, 3492, 3169, 3717, 3359, 3260, 3591,
@@ -57,6 +57,8 @@
     blk_send, blk_recv, sq_send, sq_recv, st_send, st_recv,
 ):
     z, y, c, x = (lax.axis_index(a) for a in AXES)
+    own_half = pl.ds(pl.multiple_of(c * FEAT, FEAT), FEAT)
+    other_half = pl.ds(pl.multiple_of((1 - c) * FEAT, FEAT), FEAT)
 
     def at(dx, dz, dy, dc=0):
         return (
@@ -72,8 +74,8 @@
     load.start()
 
     widened = res_ref[...].astype(jnp.float32)
-    mine = slot(0, 0, 0)
-    held[c, mine] = (widened * gain_ref[...].astype(jnp.float32)).astype(jnp.bfloat16)
+    scaled = (widened * gain_ref[...].astype(jnp.float32)).astype(jnp.bfloat16)
+    held[slot(0, 0, 0), own_half] = jnp.transpose(scaled.astype(jnp.float32)).astype(jnp.bfloat16)
     squares = jnp.sum(jnp.transpose(widened * widened), axis=0, keepdims=True)
     ssq_a[0] = jnp.broadcast_to(squares, (8, ROWS))
 
@@ -92,61 +94,64 @@
         return copy
 
     def pair_send_of(t):
-        s = slot(*offset_of(t))
-        send(held.at[c, s], held.at[c, s], pair_send.at[t], pair_recv.at[t], at(0, 0, 0, 1))
+        shard = held.at[slot(*offset_of(t)), own_half]
+        send(shard, shard, pair_send.at[t], pair_recv.at[t], at(0, 0, 0, 1))
 
     def landed(ref, sem):
         pltpu.make_async_copy(ref, ref, sem).wait()
 
     def exchange(buf, send_sem, recv_sem, places):
-        copies = [
+        return [
             send(buf.at[0], buf.at[k + 1], send_sem.at[k], recv_sem.at[k], place)
             for k, place in enumerate(places)
         ]
-        return copies
 
     plane = [at(0, 0, dy, dc) for dy in range(NY) for dc in range(2) if dy or dc]
     column = [at(0, dz, 0) for dz in range(1, NZ)]
 
-    pair_send_of(0)
+    if "pair" not in SKIP:
+        pair_send_of(0)
     acc[...] = jnp.zeros_like(acc)
-    load.wait()
 
     def multiply(g):
         dx, dz = g // 8, g % 8
         xx, zz = lax.rem(x + dx, NX), lax.rem(z + dz, NZ)
-
-        @pl.loop(0, NY)
-        def _(dy):
-            yy = lax.rem(y + dy, NY)
-            s = (xx * NZ + zz) * NY + yy
-            landed(held.at[1 - c, s], pair_recv.at[g * NY + dy])
-            both = jnp.concatenate([held[0, s], held[1, s]], axis=1)
-            start = pl.multiple_of((zz * NY + yy) * (2 * FEAT), 2 * FEAT)
-            acc[xx] += jnp.dot(
-                both, weights[pl.ds(start, 2 * FEAT), :], preferred_element_type=jnp.float32
-            )
+        if "pair" not in SKIP:
+            for dy in range(NY):
+                landed(held.at[slot(dx, dz, dy), other_half], pair_recv.at[g * NY + dy])
+        if "mm" in SKIP:
+            return
+        first = pl.multiple_of((xx * NZ + zz) * NY, NY)
+        start = pl.multiple_of(zz * (2 * NY * FEAT), 2 * NY * FEAT)
+        acc[xx] += jnp.dot(
+            weights[:, pl.ds(start, 2 * NY * FEAT)],
+            held[pl.ds(first, NY)].reshape(2 * NY * FEAT, ROWS),
+            preferred_element_type=jnp.float32,
+        )
 
     done = {dx: 0 for dx in range(NX)}
     blocks = []
-    columns_started = None
     planes_started = None
+    loaded = False
     for takes, hops, groups in plan():
         for t in takes:
-            s = slot(*offset_of(t))
-            landed(held.at[c, s], hop_recv.at[t])
-            pair_send_of(t)
+            landed(held.at[slot(*offset_of(t)), own_half], hop_recv.at[t])
+            if "pair" not in SKIP:
+                pair_send_of(t)
         for d, t in hops:
             dx, dz, dy = (a + b for a, b in zip(offset_of(t), STEPS[d]))
-            s = slot(dx, dz, dy)
-            send(held.at[c, s], held.at[c, s], hop_send.at[t], hop_recv.at[t], at(*STEPS[d]))
+            shard = held.at[slot(dx, dz, dy), own_half]
+            send(shard, shard, hop_send.at[t], hop_recv.at[t], at(*STEPS[d]))
         for g in groups:
+            if not loaded:
+                load.wait()
+                loaded = True
             multiply(g)
             if g == 0:
                 planes_started = exchange(ssq_a, sq_send.at[0], sq_recv.at[0], plane)
             dx = g // 8
             done[dx] += 1
-            if done[dx] == 8 and dx:
+            if done[dx] == 8 and dx and "blk" not in SKIP:
                 xx = lax.rem(x + dx, NX)
                 blocks.append(
                     send(acc.at[xx], logits.at[x], blk_send.at[dx - 1], blk_recv.at[dx - 1], at(dx, 0, 0))
@@ -157,31 +162,19 @@
     ssq_b[0] = jnp.sum(ssq_a[...], axis=0)
     for copy in exchange(ssq_b, sq_send.at[1], sq_recv.at[1], column):
         copy.wait()
-    inverse = lax.rsqrt(jnp.sum(ssq_b[...], axis=0) / D + 1e-05)
-
-    def to_column(lines):
-        tall = jnp.concatenate([lines] * (FEAT // 8), axis=0)
-        return jnp.transpose(tall)
-
-    inverse_column = to_column(inverse)[:, :1]
+    inverse = lax.rsqrt(jnp.sum(ssq_b[...], axis=0)[:1] / D + 1e-05)
+
     logits[x] = acc[x]
     for copy in blocks:
         copy.wait()
-
-    lane = lax.broadcasted_iota(jnp.int32, (1, COLS), 1)
-    del lane
-    highest = jnp.full((ROWS, 1), -jnp.inf, jnp.float32)
+    highest = jnp.full((1, ROWS), -jnp.inf, jnp.float32)
     for k in range(NX):
-        scaled = logits[k] * inverse_column
-        logits[k] = scaled
-        highest = jnp.maximum(highest, jnp.max(scaled, axis=1, keepdims=True))
-    total = jnp.zeros((ROWS, 1), jnp.float32)
+        highest = jnp.maximum(highest, jnp.max(logits[k] * inverse, axis=0, keepdims=True))
+    total = jnp.zeros((1, ROWS), jnp.float32)
     for k in range(NX):
-        total = total + jnp.sum(jnp.exp(logits[k] - highest), axis=1, keepdims=True)
-
-    lanes = lax.broadcasted_iota(jnp.int32, (ROWS, FEAT), 1)
-    packed = jnp.where(lanes == 0, highest, total)
-    st_a[0] = jnp.transpose(packed)[:8]
+        total = total + jnp.sum(jnp.exp(logits[k] * inverse - highest), axis=0, keepdims=True)
+
+    line = lax.broadcasted_iota(jnp.int32, (8, ROWS), 0)
 
     def merged(buf):
         top = buf[0][:1]
@@ -192,42 +185,45 @@
             add = add + buf[k][1:2] * jnp.exp(buf[k][:1] - top)
         return top, add
 
-    for copy in exchange(st_a, st_send.at[0], st_recv.at[0], plane):
-        copy.wait()
-    top, add = merged(st_a)
-    line = lax.broadcasted_iota(jnp.int32, (8, ROWS), 0)
-    st_b[0] = jnp.where(line == 0, top, add)
-    for copy in exchange(st_b, st_send.at[1], st_recv.at[1], column):
-        copy.wait()
-    top, add = merged(st_b)
-    lse = to_column(jnp.broadcast_to(top + jnp.log(add), (8, ROWS)))[:, :1]
+    if "st" not in SKIP:
+        st_a[0] = jnp.where(line == 0, highest, total)
+        for copy in exchange(st_a, st_send.at[0], st_recv.at[0], plane):
+            copy.wait()
+        top, add = merged(st_a)
+        st_b[0] = jnp.where(line == 0, top, add)
+        for copy in exchange(st_b, st_send.at[1], st_recv.at[1], column):
+            copy.wait()
+        top, add = merged(st_b)
+    else:
+        top, add = highest, total
+    lse = top + jnp.log(add)
     for k in range(NX):
-        out_ref[:, COLS * k : COLS * (k + 1)] = logits[k] - lse
-
-    @pl.loop(0, 128)
+        out_ref[COLS * k : COLS * (k + 1), :] = logits[k] * inverse - lse
+
+    @pl.loop(0 if "pair" not in SKIP else 128, 128)
     def _(t):
-        landed(held.at[c, t], pair_send.at[t])
+        landed(held.at[t, own_half], pair_send.at[t])
 
     @pl.loop(1, 128)
     def _(t):
-        landed(held.at[c, t], hop_send.at[t])
+        landed(held.at[t, own_half], hop_send.at[t])
 
 
 def local(residual, gain, unembed):
     f32, bf16 = jnp.float32, jnp.bfloat16
     vmem = pl.BlockSpec(memory_space=pltpu.VMEM)
     dma = pltpu.SemaphoreType.DMA
-    return pl.pallas_call(
+    out = pl.pallas_call(
         kernel,
         name="lens",
-        out_shape=jax.ShapeDtypeStruct((ROWS, NX * COLS), f32),
+        out_shape=jax.ShapeDtypeStruct((NX * COLS, ROWS), f32),
         in_specs=[vmem, vmem, pl.BlockSpec(memory_space=pl.ANY)],
         out_specs=vmem,
         scratch_shapes=[
-            pltpu.VMEM((2, NX * NZ * NY, ROWS, FEAT), bf16),
-            pltpu.VMEM((D, COLS), bf16),
-            pltpu.VMEM((NX, ROWS, COLS), f32),
-            pltpu.VMEM((NX, ROWS, COLS), f32),
+            pltpu.VMEM((NX * NZ * NY, 2 * FEAT, ROWS), bf16),
+            pltpu.VMEM((COLS, D), bf16),
+            pltpu.VMEM((NX, COLS, ROWS), f32),
+            pltpu.VMEM((NX, COLS, ROWS), f32),
             pltpu.VMEM((8, 8, ROWS), f32),
             pltpu.VMEM((8, 8, ROWS), f32),
             pltpu.VMEM((8, 8, ROWS), f32),
@@ -238,7 +234,8 @@
         compiler_params=pltpu.CompilerParams(
             collective_id=0, has_side_effects=True, vmem_limit_bytes=60 * 1024 * 1024
         ),
-    )(residual, gain, unembed)
+    )(residual, gain, unembed.T)
+    return out.T
 
 
 def solution(mesh):

time: 113 us -> 94.6 us (0.84)
  local copies, waits for them, and re-layouts: 14.8 us -> 3.01 us
  Pallas kernels: 97.6 us -> 91.4 us
    unnamed x1, local copies, waits for them, and re-layouts: 11.9 us -> 3.01 us
    pallas_call x1, Pallas kernels: 97.6 us -> 91.4 us  [local(): pl.pallas_call(kernel, name='lens', out_shape=jax.ShapeDtypeStruct((NX *...]
    pallas_call x1 -> x0, local copies, waits for them, and re-layouts: 2.87 us -> none  [local(): pl.pallas_call(kernel, name='lens', out_shape=jax.ShapeDtypeStruct((ROWS,...]
where the time goes in v2:
time: 94.6 us; the launch traced here: 94.5 us
  Pallas kernels  91.4 us (97%)
  local copies, waits for them, and re-layouts  3.01 us (3%)
    pallas_call x1, Pallas kernels, local(): pl.pallas_call(kernel, name='lens', out_shape=jax.ShapeDtypeStruct((NX *...  91.4 us
    unnamed x1, local copies, waits for them, and re-layouts  3.01 us

profile of v2, /device:TPU:2, one launch (start us, length us, event | category | flops | bytes accessed | tf_op | source)
XLA Modules:
  0.0 94.5 jit_solution(10055138850171760252)
XLA Ops:
  0.0 91.4 %lens.1 = f32[2004,256]{1,0:T(8,128)} custom-call(bf16[256,128]{1,0:T(8,128)(2,1)} %res_ref.1, bf16[1,128]{1,0:T(2,128)(2,1)} %gain_ref.1, bf16[501,8192]{1,0:T(8,128)(2,1)} %bitcast.2), custom_call_target="tpu_custom_call" | custom-call | tf_op jit(solution)/shard_map/lens/pallas_call | solution.py:216
  91.5 3.0 %copy.5 = f32[256,2004]{0,1:T(8,128)} copy(f32[256,2004]{0,1:T(8,128)} %bitcast.3) | data formatting | bytes 4104192

commit v3 on v2

v3 whole, which is shorter than its diff:
```python
import jax
import jax.numpy as jnp
from jax import lax
from jax.experimental import pallas as pl
from jax.experimental.pallas import tpu as pltpu
from jax.sharding import Mesh
from jax.sharding import PartitionSpec as P

D = 8192
MESH = pl.DeviceIdType.MESH
AXES = ("z", "y", "c", "x")
NX, NZ, NY = 4, 8, 4
ROWS, FEAT, COLS = 256, 128, 501

HOPS = (
    388, 284, 96, 515, 641, 160, 3619, 3809, 3236, 3452, 3172, 3463,
    4412, 4257, 4741, 4195, 4488, 4639, 5400, 5634, 5789, 5312, 6247, 6885,
    6311, 6783, 6568, 6520, 7743, 7480, 7333, 7842, 7272, 7563, 8802, 8893,
    8317, 8388, 8540, 8588, 9595, 9643, 9897, 9415, 9830, 9311, 10347, 10440,
    11001, 10732, 10612, 10811, 11692, 11838, 11480, 11357, 11572, 12009, 12966, 12717,
    12922, 12379, 12663, 12489, 13396, 13930, 13807, 13515, 14061, 13685, 14640, 14895,
    14540, 15029, 14832, 14406, 15565, 15731, 15793, 16046, 15927, 15450, 16471, 16881,
    17142, 16698, 17006, 16606, 17616, 17487, 17971, 17849, 18102, 17790, 19122, 18730,
    19058, 18517, 18641, 18832, 19795, 19534, 19601, 20185, 19914, 20054, 21189, 20756,
    20630, 21007, 20930, 20499, 22043, 21586, 21955, 21650, 21785, 22209, 22537, 23181,
    22814, 22933, 22679, 23050, 24078, 23962, 24198,
)
LAG = 3
STEPS = ((1, 0, 0), (-1, 0, 0), (0, 1, 0), (0, -1, 0), (0, 0, 1), (0, 0, -1))


SPAN = 86.5


def plan():
    arrive = {0: 0}
    for hop in HOPS:
        arrive[hop % 128] = hop // 1024 + LAG
    last = max(arrive.values())
    rounds = []
    for r in range(last + 2):
        takes = [t for t in arrive if arrive[t] == r and t != 0]
        hops = [(hop // 128 % 8, hop % 128) for hop in HOPS if hop // 1024 == r]
        groups = [
            g for g in range(32) if max(arrive[g * 4 + k] for k in range(4)) + 1 == r
        ]
        rounds.append((takes, hops, groups))
    x_last = max(hop // 1024 for hop in HOPS if hop // 128 % 8 < 2)
    came = {hop % 128: STEPS[hop // 128 % 8] for hop in HOPS}

    def moved(p, e, sign):
        return tuple((a + sign * b) % n for a, b, n in zip(p, e, (NX, NZ, NY)))

    known = {}
    for t in sorted(arrive, key=arrive.get):
        holder, p = (0, 0, 0), offset_of(t)
        shard = p
        while True:
            for near in (holder, *(moved(holder, e, 1) for e in STEPS)):
                known.setdefault(near, arrive[t])
            if holder == p:
                break
            e = came[(shard[0] * NZ + shard[1]) * NY + shard[2]]
            holder, shard = moved(holder, e, -1), moved(shard, e, 1)
    column_known = max(known[0, dz, 0] for dz in range(NZ))
    return rounds, x_last, column_known


def offset_of(t):
    return t // 32, t // 4 % 8, t % 4


def kernel(
    res_ref, gain_ref, unembed_ref, logits_ref, lse_ref,
    held, weights, acc, logits, code_out, code_in, note_out, note_in,
    ssq_a, ssq_b, ssq_c, st_a, st_b,
    w_sem, hop_send, hop_recv, pair_send, pair_recv,
    blk_send, blk_recv, note_send, note_recv, ex_send, ex_recv, out_sem,
):
    z, y, c, x = (lax.axis_index(a) for a in AXES)
    own_half = pl.ds(pl.multiple_of(c * FEAT, FEAT), FEAT)
    other_half = pl.ds(pl.multiple_of((1 - c) * FEAT, FEAT), FEAT)

    def at(dx, dz, dy, dc=0):
        return (
            lax.rem(z + dz % NZ, NZ), lax.rem(y + dy % NY, NY),
            lax.rem(c + dc, 2), lax.rem(x + dx % NX, NX),
        )

    def slot(dx, dz, dy):
        zz, yy, _, xx = at(dx, dz, dy)
        return (xx * NZ + zz) * NY + yy

    barrier = pltpu.get_barrier_semaphore()
    near = [at(*step) for step in STEPS] + [at(0, 0, 0, 1)]
    for device in near:
        pl.semaphore_signal(barrier, inc=1, device_id=device, device_id_type=MESH)
    load = pltpu.make_async_copy(unembed_ref, weights, w_sem)
    load.start()

    widened = res_ref[...].astype(jnp.float32)
    scaled = (widened * gain_ref[...].astype(jnp.float32)).astype(jnp.bfloat16)
    held[slot(0, 0, 0), own_half] = jnp.transpose(scaled.astype(jnp.float32)).astype(jnp.bfloat16)
    squares = jnp.sum(jnp.transpose(widened * widened), axis=0, keepdims=True)
    ssq_a[0] = jnp.broadcast_to(squares, (8, ROWS))
    acc[...] = jnp.zeros_like(acc)
    pl.semaphore_wait(barrier, len(near))

    def send(src, dst, send_sem, recv_sem, device):
        pltpu.make_async_remote_copy(
            src_ref=src, dst_ref=dst, send_sem=send_sem, recv_sem=recv_sem,
            device_id=device, device_id_type=MESH,
        ).start()

    def pair_send_of(t):
        shard = held.at[slot(*offset_of(t)), own_half]
        send(shard, shard, pair_send.at[t // 32], pair_recv.at[t // 4], at(0, 0, 0, 1))

    def landed(ref, sem):
        pltpu.make_async_copy(ref, ref, sem).wait()

    def exchange(buf, k, places):
        for n, place in enumerate(places):
            send(buf.at[0], buf.at[n + 1], ex_send.at[k], ex_recv.at[k], place)

    def exchanged(buf, k):
        rest = buf.at[pl.ds(1, buf.shape[0] - 1)]
        landed(rest, ex_recv.at[k])
        landed(rest, ex_send.at[k])

    plane = [at(0, 0, dy, dc) for dy in range(NY) for dc in range(2) if dy or dc]
    column = [at(0, dz, 0) for dz in range(1, NZ)]
    layers = [at(dx, 0, 0) for dx in range(1, NX)]

    def multiply(g):
        dx, dz = g // 8, g % 8
        xx, zz = lax.rem(x + dx, NX), lax.rem(z + dz, NZ)
        landed(held.at[pl.ds(0, NY), other_half], pair_recv.at[g])
        first = pl.multiple_of((xx * NZ + zz) * NY, NY)
        start = pl.multiple_of(zz * (2 * NY * FEAT), 2 * NY * FEAT)
        acc[xx] += jnp.dot(
            weights[:, pl.ds(start, 2 * NY * FEAT)],
            held[pl.ds(first, NY)].reshape(2 * NY * FEAT, ROWS),
            preferred_element_type=jnp.float32,
        )

    def inverse_of(dx):
        return lax.rsqrt(ssq_c[-dx % NX][:1] / D + 1e-05)

    def summed(values):
        highest = jnp.max(values, axis=0, keepdims=True)
        return highest, jnp.sum(jnp.exp(values - highest), axis=0, keepdims=True)

    def lines(*rows):
        line = lax.broadcasted_iota(jnp.int32, (8, ROWS), 0)
        out = jnp.broadcast_to(rows[-1], (8, ROWS))
        for k in range(len(rows) - 2, -1, -1):
            out = jnp.where(line == k, rows[k], out)
        return out

    def code_block(dx):
        values = acc[lax.rem(x + dx, NX)] * inverse_of(dx)
        highest, total = summed(values)
        reach = jnp.maximum(highest - jnp.min(values, axis=0, keepdims=True), 1e-20)
        note_out[dx - 1] = lines(highest, total, reach)
        send(note_out.at[dx - 1], note_in.at[dx - 1], note_send.at[dx - 1], note_recv.at[dx - 1], layers[dx - 1])
        step = 2 * SPAN / reach
        code_out[dx - 1] = jnp.exp(SPAN - (highest - values) * step).astype(jnp.bfloat16)

    def send_block(dx):
        send(code_out.at[dx - 1], code_in.at[dx - 1], blk_send.at[dx - 1], blk_recv.at[dx - 1], layers[dx - 1])

    pair_send_of(0)
    rounds, x_last, column_known = plan()
    whole = {dx: 0 for dx in range(NX)}
    loaded, squares_at = False, {}
    to_code, to_send = [], []
    for r, (takes, hops, groups) in enumerate(rounds):
        if takes:
            landed(held.at[pl.ds(0, len(takes)), own_half], hop_recv.at[r])
        for t in takes:
            pair_send_of(t)
        for d, t in hops:
            dx, dz, dy = (a + b for a, b in zip(offset_of(t), STEPS[d]))
            shard = held.at[slot(dx, dz, dy), own_half]
            send(shard, shard, hop_send.at[t // 32], hop_recv.at[r + LAG], at(*STEPS[d]))
        if r == squares_at.get("z"):
            exchanged(ssq_a, 0)
            ssq_b[0] = jnp.sum(ssq_a[...], axis=0)
            exchange(ssq_b, 1, column)
            squares_at["x"] = r + 4
        if r == squares_at.get("x"):
            exchanged(ssq_b, 1)
            ssq_c[0] = jnp.sum(ssq_b[...], axis=0)
            exchange(ssq_c, 2, layers)
            squares_at["done"] = r + 3
        if r == squares_at.get("done"):
            exchanged(ssq_c, 2)
        for g in groups:
            if not loaded:
                load.wait()
                loaded = True
            multiply(g)
            if g == 0:
                exchange(ssq_a, 0, plane)
                squares_at["z"] = max(r + 3, column_known)
            whole[g // 8] += 1
            if whole[g // 8] == 8 and g // 8:
                to_code.append(g // 8)
        if r >= squares_at.get("done", 1000):
            for dx in to_code:
                code_block(dx)
                to_send.append(dx)
            to_code = []
        if r >= x_last:
            for dx in to_send:
                send_block(dx)
            to_send = []
    assert not to_code and not to_send

    mine = acc[x] * inverse_of(0)
    tops, adds = [], []
    top, add = summed(mine)
    tops.append(top)
    adds.append(add)
    for k in range(NX - 1):
        landed(note_in.at[k], note_recv.at[k])
        tops.append(note_in[k][:1])
        adds.append(note_in[k][1:2])

    def merged(tops, adds):
        top = tops[0]
        for other in tops[1:]:
            top = jnp.maximum(top, other)
        add = jnp.zeros_like(top)
        for k in range(len(tops)):
            add = add + adds[k] * jnp.exp(tops[k] - top)
        return top, add

    st_a[0] = lines(*merged(tops, adds))
    exchange(st_a, 3, plane)
    logits[x] = mine
    exchanged(st_a, 3)
    st_b[0] = lines(*merged([st_a[k][:1] for k in range(8)], [st_a[k][1:2] for k in range(8)]))
    exchange(st_b, 4, column)

    for dx in (1, 3, 2):
        landed(code_in.at[dx - 1], blk_recv.at[dx - 1])
        note = note_in[dx - 1]
        highest, reach = note[:1], note[2:3]
        step = reach / (2 * SPAN)
        logits[lax.rem(x + NX - dx, NX)] = highest - (SPAN - jnp.log(code_in[dx - 1].astype(jnp.float32))) * step
    put = pltpu.make_async_copy(logits, logits_ref, out_sem)
    put.start()

    for dx in range(NX):
        landed(held.at[pl.ds(0, 32), own_half], pair_send.at[dx])
        landed(held.at[pl.ds(0, 31 if dx == 0 else 32), own_half], hop_send.at[dx])
    for k in range(NX - 1):
        landed(note_out.at[k], note_send.at[k])
        landed(code_out.at[k], blk_send.at[k])

    exchanged(st_b, 4)
    top, add = merged([st_b[k][:1] for k in range(8)], [st_b[k][1:2] for k in range(8)])
    lse_ref[...] = jnp.broadcast_to(top + jnp.log(add), (8, ROWS))
    put.wait()


def subtract(logits_ref, lse_ref, out_ref):
    lse = lse_ref[:1]
    for k in range(NX):
        out_ref[COLS * k : COLS * (k + 1), :] = logits_ref[k] - lse


def local(residual, gain, unembed):
    f32, bf16 = jnp.float32, jnp.bfloat16
    vmem = pl.BlockSpec(memory_space=pltpu.VMEM)
    anywhere = pl.BlockSpec(memory_space=pl.ANY)
    dma = pltpu.SemaphoreType.DMA
    logits, lse = pl.pallas_call(
        kernel,
        name="lens",
        out_shape=(
            jax.ShapeDtypeStruct((NX, COLS, ROWS), f32),
            jax.ShapeDtypeStruct((8, ROWS), f32),
        ),
        in_specs=[vmem, vmem, anywhere],
        out_specs=(anywhere, vmem),
        scratch_shapes=[
            pltpu.VMEM((NX * NZ * NY, 2 * FEAT, ROWS), bf16),
            pltpu.VMEM((COLS, D), bf16),
            pltpu.VMEM((NX, COLS, ROWS), f32),
            pltpu.VMEM((NX, COLS, ROWS), f32),
            pltpu.VMEM((NX - 1, COLS, ROWS), bf16),
            pltpu.VMEM((NX - 1, COLS, ROWS), bf16),
            pltpu.VMEM((NX - 1, 8, ROWS), f32),
            pltpu.VMEM((NX - 1, 8, ROWS), f32),
            pltpu.VMEM((8, 8, ROWS), f32),
            pltpu.VMEM((8, 8, ROWS), f32),
            pltpu.VMEM((NX, 8, ROWS), f32),
            pltpu.VMEM((8, 8, ROWS), f32),
            pltpu.VMEM((8, 8, ROWS), f32),
            dma, dma((4,)), dma((len(plan()[0]),)), dma((4,)), dma((32,)),
            dma((3,)), dma((3,)), dma((3,)), dma((3,)), dma((5,)), dma((5,)), dma,
        ],
        compiler_params=pltpu.CompilerParams(
            collective_id=0, has_side_effects=True, vmem_limit_bytes=58 * 1024 * 1024
        ),
    )(residual, gain, unembed.T)
    out = pl.pallas_call(
        subtract,
        name="subtract",
        out_shape=jax.ShapeDtypeStruct((NX * COLS, ROWS), f32),
        in_specs=[vmem, vmem],
        out_specs=vmem,
        compiler_params=pltpu.CompilerParams(vmem_limit_bytes=8 * 1024 * 1024),
    )(logits, lse)
    return out.T


def solution(mesh):
    torus = Mesh(mesh.devices.reshape(NZ, NY, 2, mesh.shape["layer"]), AXES)
    planes = ("z", "y", "c")
    return jax.shard_map(
        local,
        mesh=torus,
        in_specs=(P("x", planes), P(None, planes), P(None, (*planes, "x"))),
        out_specs=P("x", planes),
        check_vma=False,
    )
```

time: 94.6 us -> 71.2 us (0.75); the launches traced: 94.5 us -> 69.8 us
  Pallas kernels: 91.4 us -> 67.5 us
    pallas_call x1 -> x2, Pallas kernels: 91.4 us -> 67.5 us  [the longest x1 66 us: local(): pl.pallas_call(kernel, name='lens', out_shape=(jax.ShapeDtypeStruct((NX,...]
    unnamed x1 -> x4, local copies, waits for them, and re-layouts: 3.01 us -> 2.27 us
where the time goes in v3:
time: 71.2 us; the launch traced here: 69.8 us
  Pallas kernels  67.5 us (95%)
  local copies, waits for them, and re-layouts  2.27 us (3%)
    pallas_call x1, Pallas kernels, local(): pl.pallas_call(kernel, name='lens', out_shape=(jax.ShapeDtypeStruct((NX,...  66 us
    unnamed x4, local copies, waits for them, and re-layouts  2.27 us
    pallas_call x1, Pallas kernels, local(): pl.pallas_call(subtract, name='subtract', out_shape=jax.ShapeDtypeStruct(...  1.49 us

profile of v3, /device:TPU:2, one launch (start us, length us, event | category | flops | bytes accessed | tf_op | source)
XLA Modules:
  0.0 69.8 jit_solution(9247609063839842709)
XLA Ops:
  0.0 66.0 %lens.1 = (f32[4,501,256]{2,1,0:T(8,128)}, f32[8,256]{1,0:T(8,128)}) custom-call(bf16[256,128]{1,0:T(8,128)(2,1)} %res_ref.1, bf16[1,128]{1,0:T(2,128)(2,1)} %gain_ref.1, bf16[501,8192]{1,0:T(8,128)(2,1)} %bitcast.2), custom_call_target="tpu_custom_call" | custom-call | tf_op jit(solution)/shard_map/lens/pallas_call | solution.py:280
  66.1 0.0 copy-start
  66.1 1.6 %copy-done = f32[4,501,256]{2,1,0:T(8,128)S(1)} copy-done((f32[4,501,256]{2,1,0:T(8,128)S(1)}, f32[4,501,256]{2,1,0:T(8,128)}, u32[]{:S(2)}) %copy-start) | copy-done | bytes 2052120
  67.6 0.0 copy-start.1
  67.6 0.7 copy-done.1
  68.3 1.5 %subtract.1 = f32[2004,256]{1,0:T(8,128)} custom-call(f32[4,501,256]{2,1,0:T(8,128)S(1)} %copy-done, f32[8,256]{1,0:T(8,128)S(1)} %copy-done.1), custom_call_target="tpu_custom_call" | custom-call | tf_op jit(solution)/shard_map/subtract/pallas_call | solution.py:310
Async XLA Ops:
  66.1 1.6 %copy-start = (f32[4,501,256]{2,1,0:T(8,128)S(1)}, f32[4,501,256]{2,1,0:T(8,128)}, u32[]{:S(2)}) copy-start(f32[4,501,256]{2,1,0:T(8,128)} %get-tuple-element.7.logits_ref) | copy-start | bytes 6156292
  67.6 0.7 copy-start.1

commit v4 on v3

v4 whole, which is shorter than its diff:
```python
import jax
import jax.numpy as jnp
from jax import lax
from jax.experimental import pallas as pl
from jax.experimental.pallas import tpu as pltpu
from jax.sharding import Mesh
from jax.sharding import PartitionSpec as P

D = 8192
MESH = pl.DeviceIdType.MESH
AXES = ("z", "y", "c", "x")
NX, NZ, NY = 4, 8, 4
ROWS, FEAT, COLS = 256, 128, 501

HOPS = (
    132376, 132488, 65820, 65632, 65696, 65924, 66177, 66051, 69155, 68769, 69345, 68988,
    68707, 69028, 69732, 69948, 70274, 70175, 69824, 70023, 71052, 71305, 70824, 71195,
    70760, 70932, 71800, 71999, 71864, 72418, 72167, 72226, 73085, 73445, 72831, 73255,
    72899, 73125, 73897, 74156, 74283, 74045, 74473, 73851, 75174, 75070, 75449, 75371,
    74939, 74868, 76518, 76268, 75956, 76414, 76153, 75842, 77175, 77293, 77485, 77003,
    77354, 76869, 77915, 78319, 78138, 78458, 78570, 78022, 79279, 79152, 78943, 79415,
    79605, 79070, 79949, 80369, 80243, 80558, 80074, 80502, 81646, 80975, 81329, 81498,
    81097, 81206, 82416, 82229, 82135, 82005, 82483, 82631, 83698, 83378, 83027, 83532,
    83150, 83292, 84433, 84673, 84054, 84185, 84247, 84573, 85200, 85716, 85278, 85444,
    85576, 85080, 86677, 86482, 86543, 86158, 86288, 86038, 87186, 87046, 87578, 87315,
    87435, 87690, 88349, 88717, 88453, 89361, 89497,
)
LAG = 3
STEPS = ((1, 0, 0), (-1, 0, 0), (0, 1, 0), (0, -1, 0), (0, 0, 1), (0, 0, -1))


SPAN = 86.5
SPLIT = 304


def parts_of(hop):
    links, r, d, t = hop // 65536, hop // 1024 % 64, hop // 128 % 8, hop % 128
    return links, r, d, t, tuple(links * a for a in STEPS[d])


def plan():
    arrive = {0: 0}
    for hop in HOPS:
        links, r, _, t, _ = parts_of(hop)
        arrive[t] = r + links - 1 + LAG
    last = max(arrive.values())
    rounds = []
    for r in range(last + 2):
        takes = [t for t in arrive if arrive[t] == r]
        hops = [(parts_of(hop)[4], hop % 128, arrive[hop % 128]) for hop in HOPS if parts_of(hop)[1] == r]
        rounds.append((takes, hops))
    x_last = max(parts_of(hop)[1] for hop in HOPS if parts_of(hop)[2] < 2)
    came = {hop % 128: parts_of(hop)[4] for hop in HOPS}

    def moved(p, e, sign):
        return tuple((a + sign * b) % n for a, b, n in zip(p, e, (NX, NZ, NY)))

    known, passed = {}, {}
    for t in sorted(arrive, key=arrive.get):
        holder, p = (0, 0, 0), offset_of(t)
        shard = p
        while True:
            passed.setdefault(holder, arrive[t])
            for near in (holder, *(moved(holder, e, 1) for e in STEPS)):
                known.setdefault(near, arrive[t])
            if holder == p:
                break
            e = came[(shard[0] * NZ + shard[1]) * NY + shard[2]]
            holder, shard = moved(holder, e, -1), moved(shard, e, 1)
    column_known = max(known[0, dz, 0] for dz in range(NZ))
    plane_known = max(passed[0, 0, dy] for dy in range(NY))
    return rounds, x_last, plane_known, column_known


def offset_of(t):
    return t // 32, t // 4 % 8, t % 4


def kernel(
    res_ref, gain_ref, unembed_ref, logits_ref, lse_ref,
    held, weights, acc, logits, code_out, code_in, passed, note_out, note_in,
    ssq_a, ssq_b, ssq_c, st_a, st_b,
    w_sem, hop_send, hop_recv, pair_send, pair_recv,
    blk_send, blk_recv, note_send, note_recv, ex_send, ex_recv, out_sem,
):
    z, y, c, x = (lax.axis_index(a) for a in AXES)
    own_half = pl.ds(pl.multiple_of(c * FEAT, FEAT), FEAT)
    other_half = pl.ds(pl.multiple_of((1 - c) * FEAT, FEAT), FEAT)

    def at(dx, dz, dy, dc=0):
        return (
            lax.rem(z + dz % NZ, NZ), lax.rem(y + dy % NY, NY),
            lax.rem(c + dc, 2), lax.rem(x + dx % NX, NX),
        )

    def slot(dx, dz, dy):
        zz, yy, _, xx = at(dx, dz, dy)
        return (xx * NZ + zz) * NY + yy

    barrier = pltpu.get_barrier_semaphore()
    near = [at(*step) for step in STEPS] + [at(0, 0, 0, 1), at(0, 2, 0), at(0, -2, 0)]
    for device in near:
        pl.semaphore_signal(barrier, inc=1, device_id=device, device_id_type=MESH)
    load = pltpu.make_async_copy(unembed_ref, weights, w_sem)
    load.start()

    widened = res_ref[...].astype(jnp.float32)
    scaled = (widened * gain_ref[...].astype(jnp.float32)).astype(jnp.bfloat16)
    held[slot(0, 0, 0), own_half] = jnp.transpose(scaled.astype(jnp.float32)).astype(jnp.bfloat16)
    squares = jnp.sum(jnp.transpose(widened * widened), axis=0, keepdims=True)
    ssq_a[0] = squares
    acc[...] = jnp.zeros_like(acc)
    pl.semaphore_wait(barrier, len(near))

    def send(src, dst, send_sem, recv_sem, device):
        pltpu.make_async_remote_copy(
            src_ref=src, dst_ref=dst, send_sem=send_sem, recv_sem=recv_sem,
            device_id=device, device_id_type=MESH,
        ).start()

    def pair_send_of(t, r):
        shard = held.at[slot(*offset_of(t)), own_half]
        send(shard, shard, pair_send.at[t // 32], pair_recv.at[r], at(0, 0, 0, 1))

    def landed(ref, sem):
        pltpu.make_async_copy(ref, ref, sem).wait()

    def exchange(buf, k, places):
        for n, place in enumerate(places):
            send(buf.at[0], buf.at[n + 1], ex_send.at[k], ex_recv.at[k], place)

    def exchanged(buf, k):
        rest = buf.at[pl.ds(1, buf.shape[0] - 1)]
        landed(rest, ex_recv.at[k])
        landed(rest, ex_send.at[k])

    plane = [at(0, 0, dy, dc) for dy in range(NY) for dc in range(2) if dy or dc]
    column = [at(0, dz, 0) for dz in range(1, NZ)]
    layers = [at(dx, 0, 0) for dx in range(1, NX)]

    def multiply(shards, r):
        landed(held.at[pl.ds(0, len(shards)), other_half], pair_recv.at[r])

        @pl.loop(0, len(shards))
        def _(n):
            t = shards[0]
            for k in range(1, len(shards)):
                t = jnp.where(n == k, shards[k], t)
            xx, zz = lax.rem(x + t // 32, NX), lax.rem(z + t // 4 % NZ, NZ)
            yy = lax.rem(y + t % NY, NY)
            start = pl.multiple_of((zz * NY + yy) * (2 * FEAT), 2 * FEAT)
            acc[xx] += jnp.dot(
                weights[:, pl.ds(start, 2 * FEAT)],
                held[(xx * NZ + zz) * NY + yy],
                preferred_element_type=jnp.float32,
            )

    def inverse_of(dx):
        return lax.rsqrt(ssq_c[-dx % NX] / D + 1e-05)

    def summed(values):
        highest = jnp.max(values, axis=0, keepdims=True)
        return highest, jnp.sum(jnp.exp(values - highest), axis=0, keepdims=True)

    def lines(*rows):
        count = 2 if len(rows) == 2 else 4
        line = lax.broadcasted_iota(jnp.int32, (count, ROWS), 0)
        out = jnp.broadcast_to(rows[-1], (count, ROWS))
        for k in range(len(rows) - 2, -1, -1):
            out = jnp.where(line == k, rows[k], out)
        return out

    def code_block(dx):
        values = acc[lax.rem(x + dx, NX)] * inverse_of(dx)
        highest, total = summed(values)
        reach = jnp.maximum(highest - jnp.min(values, axis=0, keepdims=True), 1e-20)
        note_out[dx - 1] = lines(highest, total, reach)
        send(note_out.at[dx - 1], note_in.at[dx - 1], note_send.at[dx - 1], note_recv.at[dx - 1], layers[dx - 1])
        step = 2 * SPAN / reach
        code_out[dx - 1] = jnp.exp(SPAN - (highest - values) * step).astype(jnp.bfloat16)

    near_part, far_part = pl.ds(0, SPLIT), pl.ds(SPLIT, COLS - SPLIT)

    def send_block(dx):
        if dx == 2:
            send(code_out.at[1, far_part], passed, blk_send.at[3], blk_recv.at[3], at(-1, 0, 0))
            send(code_out.at[1, near_part], code_in.at[1, near_part], blk_send.at[1], blk_recv.at[1], at(2, 0, 0))
        else:
            send(code_out.at[dx - 1], code_in.at[dx - 1], blk_send.at[dx - 1], blk_recv.at[dx - 1], layers[dx - 1])

    pair_send_of(0, 0)
    rounds, x_last, plane_known, column_known = plan()
    left = {dx: 32 for dx in range(NX)}
    squares_at = {}
    to_code, to_send, ready = [], [], ()
    for r, (takes, hops) in enumerate(rounds):
        if takes and r:
            landed(held.at[pl.ds(0, len(takes)), own_half], hop_recv.at[r])
            for t in takes:
                pair_send_of(t, r)
        for way, t, lands in hops:
            shard = held.at[slot(*(a + b for a, b in zip(offset_of(t), way))), own_half]
            send(shard, shard, hop_send.at[t // 32], hop_recv.at[lands], at(*way))
        if r == squares_at.get("z"):
            exchanged(ssq_a, 0)
            ssq_b[0] = jnp.sum(ssq_a[...], axis=0)
            exchange(ssq_b, 1, column)
            squares_at["x"] = r + 5
        if r == squares_at.get("x"):
            exchanged(ssq_b, 1)
            ssq_c[0] = jnp.sum(ssq_b[...], axis=0)
            exchange(ssq_c, 2, layers)
            squares_at["done"] = r + 4
        if r == squares_at.get("done"):
            exchanged(ssq_c, 2)
        if r == 1:
            load.wait()
        if ready:
            multiply(ready, r - 1)
        for t in ready:
            left[t // 32] -= 1
            if left[t // 32] == 0 and t // 32:
                to_code.append(t // 32)
        ready = takes
        if r == plane_known:
            exchange(ssq_a, 0, plane)
            squares_at["z"] = max(r + 4, column_known)
        if r >= squares_at.get("done", 1000):
            for dx in to_code:
                code_block(dx)
                to_send.append(dx)
            to_code = []
        if r >= x_last:
            for dx in to_send:
                send_block(dx)
            to_send = []
    assert not to_code and not to_send

    mine = acc[x] * inverse_of(0)
    tops, adds = [], []
    top, add = summed(mine)
    tops.append(top)
    adds.append(add)
    for k in range(NX - 1):
        landed(note_in.at[k], note_recv.at[k])
        tops.append(note_in[k][:1])
        adds.append(note_in[k][1:2])

    def merged(tops, adds):
        top = tops[0]
        for other in tops[1:]:
            top = jnp.maximum(top, other)
        add = jnp.zeros_like(top)
        for k in range(len(tops)):
            add = add + adds[k] * jnp.exp(tops[k] - top)
        return top, add

    st_a[0] = lines(*merged(tops, adds))
    exchange(st_a, 3, plane)
    landed(passed, blk_recv.at[3])
    send(passed, code_in.at[1, far_part], blk_send.at[4], blk_recv.at[4], at(-1, 0, 0))
    logits[x] = mine
    exchanged(st_a, 3)
    st_b[0] = lines(*merged([st_a[k][:1] for k in range(8)], [st_a[k][1:2] for k in range(8)]))
    exchange(st_b, 4, column)

    for dx in (1, 3, 2):
        if dx == 2:
            landed(code_in.at[1, near_part], blk_recv.at[1])
            landed(code_in.at[1, far_part], blk_recv.at[4])
        else:
            landed(code_in.at[dx - 1], blk_recv.at[dx - 1])
        note = note_in[dx - 1]
        highest, reach = note[:1], note[2:3]
        step = reach / (2 * SPAN)
        logits[lax.rem(x + NX - dx, NX)] = highest - (SPAN - jnp.log(code_in[dx - 1].astype(jnp.float32))) * step
    put = pltpu.make_async_copy(logits, logits_ref, out_sem)
    put.start()

    for dx in range(NX):
        landed(held.at[pl.ds(0, 32), own_half], pair_send.at[dx])
        landed(held.at[pl.ds(0, 31 if dx == 0 else 32), own_half], hop_send.at[dx])
    for k in range(NX - 1):
        landed(note_out.at[k], note_send.at[k])
        if k != 1:
            landed(code_out.at[k], blk_send.at[k])
    landed(code_out.at[1, near_part], blk_send.at[1])
    landed(passed, blk_send.at[3])
    landed(passed, blk_send.at[4])

    exchanged(st_b, 4)
    top, add = merged([st_b[k][:1] for k in range(8)], [st_b[k][1:2] for k in range(8)])
    lse_ref[...] = jnp.broadcast_to(top + jnp.log(add), (8, ROWS))
    put.wait()


def subtract(logits_ref, lse_ref, out_ref):
    lse = lse_ref[:1]
    for k in range(NX):
        out_ref[COLS * k : COLS * (k + 1), :] = logits_ref[k] - lse


def local(residual, gain, unembed):
    f32, bf16 = jnp.float32, jnp.bfloat16
    vmem = pl.BlockSpec(memory_space=pltpu.VMEM)
    anywhere = pl.BlockSpec(memory_space=pl.ANY)
    dma = pltpu.SemaphoreType.DMA
    logits, lse = pl.pallas_call(
        kernel,
        name="lens",
        out_shape=(
            jax.ShapeDtypeStruct((NX, COLS, ROWS), f32),
            jax.ShapeDtypeStruct((8, ROWS), f32),
        ),
        in_specs=[vmem, vmem, anywhere],
        out_specs=(anywhere, vmem),
        scratch_shapes=[
            pltpu.VMEM((NX * NZ * NY, 2 * FEAT, ROWS), bf16),
            pltpu.VMEM((COLS, D), bf16),
            pltpu.VMEM((NX, COLS, ROWS), f32),
            pltpu.VMEM((NX, COLS, ROWS), f32),
            pltpu.VMEM((NX - 1, COLS, ROWS), bf16),
            pltpu.VMEM((NX - 1, COLS, ROWS), bf16),
            pltpu.VMEM((COLS - SPLIT, ROWS), bf16),
            pltpu.VMEM((NX - 1, 4, ROWS), f32),
            pltpu.VMEM((NX - 1, 4, ROWS), f32),
            pltpu.VMEM((8, 1, ROWS), f32),
            pltpu.VMEM((8, 1, ROWS), f32),
            pltpu.VMEM((NX, 1, ROWS), f32),
            pltpu.VMEM((8, 2, ROWS), f32),
            pltpu.VMEM((8, 2, ROWS), f32),
            dma, dma((4,)), dma((len(plan()[0]),)), dma((4,)), dma((len(plan()[0]),)),
            dma((5,)), dma((5,)), dma((3,)), dma((3,)), dma((5,)), dma((5,)), dma,
        ],
        compiler_params=pltpu.CompilerParams(
            collective_id=0, has_side_effects=True, vmem_limit_bytes=50 * 1024 * 1024
        ),
    )(residual, gain, unembed.T)
    out = pl.pallas_call(
        subtract,
        name="subtract",
        out_shape=jax.ShapeDtypeStruct((NX * COLS, ROWS), f32),
        in_specs=[vmem, vmem],
        out_specs=vmem,
        compiler_params=pltpu.CompilerParams(vmem_limit_bytes=8 * 1024 * 1024),
    )(logits, lse)
    return out.T


def solution(mesh):
    torus = Mesh(mesh.devices.reshape(NZ, NY, 2, mesh.shape["layer"]), AXES)
    planes = ("z", "y", "c")
    return jax.shard_map(
        local,
        mesh=torus,
        in_specs=(P("x", planes), P(None, planes), P(None, (*planes, "x"))),
        out_specs=P("x", planes),
        check_vma=False,
    )
```

time: 71.2 us -> 63.9 us (0.90)
  Pallas kernels: 67.5 us -> 61.1 us
  local copies, waits for them, and re-layouts: 2.27 us -> 1.49 us
    pallas_call x1, Pallas kernels: 66 us -> 59.6 us  [local(): pl.pallas_call(kernel, name='lens', out_shape=(jax.ShapeDtypeStruct((NX,...]
    unnamed x4, local copies, waits for them, and re-layouts: 2.27 us -> 1.49 us
where the time goes in v4:
time: 63.9 us; the launch traced here: 62.6 us
  Pallas kernels  61.1 us (96%)
  local copies, waits for them, and re-layouts  1.49 us (2%)
    pallas_call x1, Pallas kernels, local(): pl.pallas_call(kernel, name='lens', out_shape=(jax.ShapeDtypeStruct((NX,...  59.6 us
    unnamed x4, local copies, waits for them, and re-layouts  1.49 us
    pallas_call x1, Pallas kernels, local(): pl.pallas_call(subtract, name='subtract', out_shape=jax.ShapeDtypeStruct(...  1.49 us

profile of v4, /device:TPU:2, one launch (start us, length us, event | category | flops | bytes accessed | tf_op | source)
XLA Modules:
  0.0 62.6 jit_solution(2147867670924264672)
XLA Ops:
  0.0 0.0 copy-start
  0.0 0.8 %copy-done = bf16[256,128]{1,0:T(8,128)(2,1)S(1)} copy-done((bf16[256,128]{1,0:T(8,128)(2,1)S(1)}, bf16[256,128]{1,0:T(8,128)(2,1)}, u32[]{:S(2)}) %copy-start) | copy-done | bytes 65560
  0.8 0.0 copy-start.1
  0.8 0.7 %copy-done.1 = bf16[1,128]{1,0:T(2,128)(2,1)S(1)} copy-done((bf16[1,128]{1,0:T(2,128)(2,1)S(1)}, bf16[1,128]{1,0:T(2,128)(2,1)}, u32[]{:S(2)}) %copy-start.1) | copy-done | bytes 280
  1.5 59.6 %lens.1 = (f32[4,501,256]{2,1,0:T(8,128)S(1)}, f32[8,256]{1,0:T(8,128)S(1)}) custom-call(bf16[256,128]{1,0:T(8,128)(2,1)S(1)} %copy-done, bf16[1,128]{1,0:T(2,128)(2,1)S(1)} %copy-done.1, bf16[501,8192]{1,0:T(8,128)(2,1)} %bitcast.2), custom_call_target="tpu_custom_call" | custom-call | tf_op jit(solution)/shard_map/lens/pallas_call | solution.py:308
  61.1 1.5 %subtract.1 = f32[2004,256]{1,0:T(8,128)} custom-call(f32[4,501,256]{2,1,0:T(8,128)S(1)} %get-tuple-element.7.logits_ref, f32[8,256]{1,0:T(8,128)S(1)} %get-tuple-element.8.lse_ref), custom_call_target="tpu_custom_call" | custom-call | tf_op jit(solution)/shard_map/subtract/pallas_call | solution.py:339
Async XLA Ops:
  0.0 0.8 %copy-start = (bf16[256,128]{1,0:T(8,128)(2,1)S(1)}, bf16[256,128]{1,0:T(8,128)(2,1)}, u32[]{:S(2)}) copy-start(bf16[256,128]{1,0:T(8,128)(2,1)} %res_ref.1) | copy-start | bytes 196612
  0.8 0.7 %copy-start.1 = (bf16[1,128]{1,0:T(2,128)(2,1)S(1)}, bf16[1,128]{1,0:T(2,128)(2,1)}, u32[]{:S(2)}) copy-start(bf16[1,128]{1,0:T(2,128)(2,1)} %gain_ref.1) | copy-start | bytes 772

commit v5 on v4

--- a/solution.py
+++ b/solution.py
@@ -78,10 +78,10 @@
 
 def kernel(
     res_ref, gain_ref, unembed_ref, logits_ref, lse_ref,
-    held, weights, acc, logits, code_out, code_in, passed, note_out, note_in,
+    res, gain, held, weights, acc, code_out, code_in, passed, note_out, note_in,
     ssq_a, ssq_b, ssq_c, st_a, st_b,
     w_sem, hop_send, hop_recv, pair_send, pair_recv,
-    blk_send, blk_recv, note_send, note_recv, ex_send, ex_recv, out_sem,
+    blk_send, blk_recv, note_send, note_recv, ex_send, ex_recv, out_sem, in_sem,
 ):
     z, y, c, x = (lax.axis_index(a) for a in AXES)
     own_half = pl.ds(pl.multiple_of(c * FEAT, FEAT), FEAT)
@@ -101,11 +101,18 @@
     near = [at(*step) for step in STEPS] + [at(0, 0, 0, 1), at(0, 2, 0), at(0, -2, 0)]
     for device in near:
         pl.semaphore_signal(barrier, inc=1, device_id=device, device_id_type=MESH)
+    brought = [
+        pltpu.make_async_copy(res_ref, res, in_sem.at[0]),
+        pltpu.make_async_copy(gain_ref, gain, in_sem.at[1]),
+    ]
     load = pltpu.make_async_copy(unembed_ref, weights, w_sem)
-    load.start()
-
-    widened = res_ref[...].astype(jnp.float32)
-    scaled = (widened * gain_ref[...].astype(jnp.float32)).astype(jnp.bfloat16)
+    for copy in (*brought, load):
+        copy.start()
+
+    for copy in brought:
+        copy.wait()
+    widened = res[...].astype(jnp.float32)
+    scaled = (widened * gain[...].astype(jnp.float32)).astype(jnp.bfloat16)
     held[slot(0, 0, 0), own_half] = jnp.transpose(scaled.astype(jnp.float32)).astype(jnp.bfloat16)
     squares = jnp.sum(jnp.transpose(widened * widened), axis=0, keepdims=True)
     ssq_a[0] = squares
@@ -259,7 +266,12 @@
     exchange(st_a, 3, plane)
     landed(passed, blk_recv.at[3])
     send(passed, code_in.at[1, far_part], blk_send.at[4], blk_recv.at[4], at(-1, 0, 0))
-    logits[x] = mine
+    puts = []
+
+    def put(k, values):
+        logits_ref[k] = values
+
+    put(x, mine)
     exchanged(st_a, 3)
     st_b[0] = lines(*merged([st_a[k][:1] for k in range(8)], [st_a[k][1:2] for k in range(8)]))
     exchange(st_b, 4, column)
@@ -273,9 +285,8 @@
         note = note_in[dx - 1]
         highest, reach = note[:1], note[2:3]
         step = reach / (2 * SPAN)
-        logits[lax.rem(x + NX - dx, NX)] = highest - (SPAN - jnp.log(code_in[dx - 1].astype(jnp.float32))) * step
-    put = pltpu.make_async_copy(logits, logits_ref, out_sem)
-    put.start()
+        values = highest - (SPAN - jnp.log(code_in[dx - 1].astype(jnp.float32))) * step
+        put(lax.rem(x + NX - dx, NX), values)
 
     for dx in range(NX):
         landed(held.at[pl.ds(0, 32), own_half], pair_send.at[dx])
@@ -291,19 +302,28 @@
     exchanged(st_b, 4)
     top, add = merged([st_b[k][:1] for k in range(8)], [st_b[k][1:2] for k in range(8)])
     lse_ref[...] = jnp.broadcast_to(top + jnp.log(add), (8, ROWS))
-    put.wait()
-
-
-def subtract(logits_ref, lse_ref, out_ref):
-    lse = lse_ref[:1]
+    for copy in puts:
+        copy.wait()
+
+
+def subtract(logits_ref, lse_ref, out_ref, out, out_sem):
+    writes, begin = [], 0
     for k in range(NX):
-        out_ref[COLS * k : COLS * (k + 1), :] = logits_ref[k] - lse
+        out[COLS * k : COLS * (k + 1), :] = logits_ref[k] - lse_ref[:1]
+        end = COLS * (k + 1) if k == NX - 1 else COLS * (k + 1) // 8 * 8
+        rows = pl.ds(begin, end - begin)
+        writes.append(pltpu.make_async_copy(out.at[rows], out_ref.at[rows], out_sem.at[k]))
+        writes[-1].start()
+        begin = end
+    for copy in writes:
+        copy.wait()
 
 
 def local(residual, gain, unembed):
     f32, bf16 = jnp.float32, jnp.bfloat16
     vmem = pl.BlockSpec(memory_space=pltpu.VMEM)
     anywhere = pl.BlockSpec(memory_space=pl.ANY)
+    hbm = pl.BlockSpec(memory_space=pltpu.HBM)
     dma = pltpu.SemaphoreType.DMA
     logits, lse = pl.pallas_call(
         kernel,
@@ -312,12 +332,13 @@
             jax.ShapeDtypeStruct((NX, COLS, ROWS), f32),
             jax.ShapeDtypeStruct((8, ROWS), f32),
         ),
-        in_specs=[vmem, vmem, anywhere],
-        out_specs=(anywhere, vmem),
+        in_specs=[hbm, hbm, hbm],
+        out_specs=(vmem, vmem),
         scratch_shapes=[
+            pltpu.VMEM((ROWS, FEAT), bf16),
+            pltpu.VMEM((1, FEAT), bf16),
             pltpu.VMEM((NX * NZ * NY, 2 * FEAT, ROWS), bf16),
             pltpu.VMEM((COLS, D), bf16),
-            pltpu.VMEM((NX, COLS, ROWS), f32),
             pltpu.VMEM((NX, COLS, ROWS), f32),
             pltpu.VMEM((NX - 1, COLS, ROWS), bf16),
             pltpu.VMEM((NX - 1, COLS, ROWS), bf16),
@@ -330,7 +351,7 @@
             pltpu.VMEM((8, 2, ROWS), f32),
             pltpu.VMEM((8, 2, ROWS), f32),
             dma, dma((4,)), dma((len(plan()[0]),)), dma((4,)), dma((len(plan()[0]),)),
-            dma((5,)), dma((5,)), dma((3,)), dma((3,)), dma((5,)), dma((5,)), dma,
+            dma((5,)), dma((5,)), dma((3,)), dma((3,)), dma((5,)), dma((5,)), dma((NX,)), dma((2,)),
         ],
         compiler_params=pltpu.CompilerParams(
             collective_id=0, has_side_effects=True, vmem_limit_bytes=50 * 1024 * 1024
@@ -341,7 +362,8 @@
         name="subtract",
         out_shape=jax.ShapeDtypeStruct((NX * COLS, ROWS), f32),
         in_specs=[vmem, vmem],
-        out_specs=vmem,
+        out_specs=anywhere,
+        scratch_shapes=[pltpu.VMEM((NX * COLS, ROWS), f32), dma((NX,))],
         compiler_params=pltpu.CompilerParams(vmem_limit_bytes=8 * 1024 * 1024),
     )(logits, lse)
     return out.T

time: 63.9 us -> 63.8 us (level)
  no operation moved by 1% of the time
where the time goes in v5:
time: 63.8 us; the launch traced here: 62.5 us
  Pallas kernels  61 us (96%)
  local copies, waits for them, and re-layouts  1.49 us (2%)
    pallas_call x1, Pallas kernels, local(): pl.pallas_call(kernel, name='lens', out_shape=(jax.ShapeDtypeStruct((NX,...  59.6 us
    unnamed x4, local copies, waits for them, and re-layouts  1.49 us
    pallas_call x1, Pallas kernels, local(): pl.pallas_call(subtract, name='subtract', out_shape=jax.ShapeDtypeStruct(...  1.37 us

profile of v5, /device:TPU:2, one launch (start us, length us, event | category | flops | bytes accessed | tf_op | source)
XLA Modules:
  0.0 62.5 jit_solution(10353460360686054819)
XLA Ops:
  0.0 0.0 copy-start
  0.0 0.8 %copy-done = bf16[256,128]{1,0:T(8,128)(2,1)S(1)} copy-done((bf16[256,128]{1,0:T(8,128)(2,1)S(1)}, bf16[256,128]{1,0:T(8,128)(2,1)}, u32[]{:S(2)}) %copy-start) | copy-done | bytes 65560
  0.8 0.0 copy-start.1
  0.8 0.7 %copy-done.1 = bf16[1,128]{1,0:T(2,128)(2,1)S(1)} copy-done((bf16[1,128]{1,0:T(2,128)(2,1)S(1)}, bf16[1,128]{1,0:T(2,128)(2,1)}, u32[]{:S(2)}) %copy-start.1) | copy-done | bytes 280
  1.5 59.6 %lens.1 = (f32[4,501,256]{2,1,0:T(8,128)S(1)}, f32[8,256]{1,0:T(8,128)S(1)}) custom-call(bf16[256,128]{1,0:T(8,128)(2,1)S(1)} %copy-done, bf16[1,128]{1,0:T(2,128)(2,1)S(1)} %copy-done.1, bf16[501,8192]{1,0:T(8,128)(2,1)} %bitcast.2), custom_call_target="tpu_custom_call" | custom-call | tf_op jit(solution)/shard_map/lens/pallas_call | solution.py:328
  61.2 1.4 %subtract.1 = f32[2004,256]{1,0:T(8,128)} custom-call(f32[4,501,256]{2,1,0:T(8,128)S(1)} %get-tuple-element.7.logits_ref, f32[8,256]{1,0:T(8,128)S(1)} %get-tuple-element.8.lse_ref), custom_call_target="tpu_custom_call" | custom-call | tf_op jit(solution)/shard_map/subtract/pallas_call | solution.py:360
Async XLA Ops:
  0.0 0.8 %copy-start = (bf16[256,128]{1,0:T(8,128)(2,1)S(1)}, bf16[256,128]{1,0:T(8,128)(2,1)}, u32[]{:S(2)}) copy-start(bf16[256,128]{1,0:T(8,128)(2,1)} %res_ref.1) | copy-start | bytes 196612
  0.8 0.7 %copy-start.1 = (bf16[1,128]{1,0:T(2,128)(2,1)S(1)}, bf16[1,128]{1,0:T(2,128)(2,1)}, u32[]{:S(2)}) copy-start(bf16[1,128]{1,0:T(2,128)(2,1)} %gain_ref.1) | copy-start | bytes 772
